TPU v7x, 32 devices: a whole 2x2x4 slice. The times are simulated.
32 devices in a mesh: gx: 4 (over y, x), gy: 4 (over z), gz: 2 (over core).
Axes of the slice: x: 2, y: 2, z: 4, core: 2. Of those that a mesh axis runs over, the one named last changes fastest.
Arguments:
- right_side: float32 [5, 512, 8, 128], P(None, ('gx', 'gy', 'gz')), may hold values from -6 to 6
- diag_inverse: bfloat16 [5, 512, 128, 128], P(None, ('gx', 'gy', 'gz')), may hold values from -0.5 to 0.5
- off_blocks: bfloat16 [4, 1024, 128, 128], P(None, ('gx', 'gy', 'gz')), may hold values from -0.375 to 0.375
- live_counts: int32 [5, 32], P(None, ('gx', 'gy', 'gz')), may hold values from 1 to 16, as said below
- source_slot: int32 [4, 1024], P(None, ('gx', 'gy', 'gz')), may hold values from 0 to 15, as said below
- target_owner: int32 [4, 1024], P(None, ('gx', 'gy', 'gz')), may hold values from 0 to 31, as said below
- target_block: int32 [4, 1024], P(None, ('gx', 'gy', 'gz')), may hold values from 16 to 79, as said below
Outputs:
- solution: float32 [5, 512, 8, 128], P(None, ('gx', 'gy', 'gz'))
Inputs may be any that keep to these rules, and one draw needn't show every extreme that they name: `live_counts`: slots at or past a device's count in a level are empty; in every level some device has all 16 slots live. `source_slot`: names a live slot of the issuing device in the same level. `target_owner`: in every level, each device's records go exactly 2 each to 16 distinct owners and none to the others. `target_block`: the level part is later than the record's own level, and the slot is live at the owner in that level.
All inputs are finite; a program needn't handle non-finite values.
Results may differ from a plain program's by a relative error of at most 0.013.
Values sent between devices are 32-bit elements; how exact they have to be, the bound alone decides.
A program may use at most 64 MiB of HBM per device.

v0:
```python
import functools

import jax
import jax.numpy as jnp
from jax import lax
from jax.experimental import pallas as pl
from jax.experimental.pallas import tpu as pltpu
from jax.sharding import PartitionSpec as P

CAP = 2
GROUP = 4
AXES = ("gx", "gy", "gz")
MESH = pl.DeviceIdType.MESH


def kernel(
    sizes,
    live_ref,
    source_ref,
    owner_ref,
    block_ref,
    right_hbm,
    diag_hbm,
    off_hbm,
    out_hbm,
    work_ref,
    diag_ref,
    off_refs,
    solved_ref,
    outgoing_ref,
    arrived_ref,
    names_out_ref,
    names_ref,
    record_vmem,
    record_ref,
    load_sem,
    out_sem,
    record_sem,
    send_sem,
    recv_sem,
    name_send_sem,
    name_recv_sem,
):
    nx, ny, nz = sizes
    devices = nx * ny * nz
    plane = nx * nz
    levels, slots = diag_ref.shape[:2]
    records = off_refs[0].shape[0]
    rhs = solved_ref.shape[-2]
    pack = CAP * rhs
    level_rows = slots * rhs
    lanes = names_ref.shape[-1]
    mx, my, mz = (lax.axis_index(axis) for axis in AXES)
    me = (mx * ny + my) * nz + mz

    def partner(index):
        at = index // plane
        down = ny - 1 - at
        down = down - jnp.where(down > my, 0, 1)
        up = at + jnp.where(at < my, 0, 1)
        oy = jnp.where(at == ny - 1, my, jnp.where(2 * my < ny, down, up))
        rest = lax.rem(index, plane) + 1
        ox = lax.rem(mx + rest // nz, nx)
        oz = lax.rem(mz + lax.rem(rest, nz), nz)
        return (ox * ny + oy) * nz + oz, (ox, oy, oz)

    right_load = pltpu.make_async_copy(right_hbm, work_ref, load_sem.at[0])
    diag_loads = [
        pltpu.make_async_copy(diag_hbm.at[at], diag_ref.at[at], load_sem.at[1 + at])
        for at in range(levels)
    ]
    off_loads = [
        pltpu.make_async_copy(off_hbm.at[at], off_refs[at], load_sem.at[1 + levels + at])
        for at in range(levels - 1)
    ]
    barrier = pltpu.get_barrier_semaphore()

    @pl.loop(0, devices - 1)
    def _(index):
        pl.semaphore_signal(barrier, inc=1, device_id=partner(index)[1], device_id_type=MESH)

    right_load.start()
    for at in range(levels):
        diag_loads[at].start()
        if at < levels - 1:
            off_loads[at].start()

    owner_ids = lax.broadcasted_iota(jnp.int32, (devices, records), 0)
    record_ids = lax.broadcasted_iota(jnp.int32, (devices, records), 1)
    lane_ids = lax.broadcasted_iota(jnp.int32, (devices, lanes), 1)
    told = jnp.zeros((devices, lanes), jnp.float32)
    index = jnp.zeros((devices, lanes), jnp.int32)
    for at in range(levels - 1):
        hits = owner_ids == owner_ref[at : at + 1, :]
        block_row = (block_ref[at : at + 1, :] + 1).astype(jnp.float32)
        first = jnp.min(jnp.where(hits, record_ids, records - 1), axis=1, keepdims=True)
        last = jnp.max(jnp.where(hits, record_ids, 0), axis=1, keepdims=True)
        for copy_at, record in enumerate((first, last)):
            chosen = jnp.where(hits & (record_ids == record), block_row, 0.0)
            label = jnp.sum(chosen, axis=1, keepdims=True)
            told = jnp.where(lane_ids == at * CAP + copy_at, label, told)
            index = jnp.where(lane_ids == at * CAP + copy_at, record, index)
    record_vmem[...] = index
    names_out_ref[...] = told.reshape(devices, 1, lanes)
    names_ref[pl.ds(me, 1)] = names_out_ref[pl.ds(me, 1)]
    record_copy = pltpu.make_async_copy(record_vmem, record_ref, record_sem)
    record_copy.start()

    def solve(at):
        diag_loads[at].wait()
        count = live_ref[0, at]
        for slot in range(slots):
            row = (at * slots + slot) * rhs
            work = work_ref[row : row + rhs, :].astype(jnp.bfloat16)
            solved = jnp.dot(work, diag_ref[at, slot], preferred_element_type=jnp.float32)
            solved_ref[at, slot] = jnp.where(slot < count, solved, jnp.float32(0.0))
        pltpu.make_async_copy(solved_ref.at[at], out_hbm.at[at], out_sem.at[at]).start()

    def make(at, other, target_ref, base):
        for copy_at in range(CAP):
            record = record_ref[other, at * CAP + copy_at]
            picked = solved_ref[at, source_ref[at, record]].astype(jnp.bfloat16)
            target_ref[at, pl.ds(base + copy_at * rhs, rhs), :] = jnp.dot(
                picked, off_refs[at][record], preferred_element_type=jnp.float32
            )

    def make_out(at, index):
        other, _ = partner(index)
        make(at, other, outgoing_ref, other * pack)

    def send(at, index):
        other, where = partner(index)
        pltpu.make_async_remote_copy(
            src_ref=outgoing_ref.at[at, pl.ds(other * pack, pack)],
            dst_ref=arrived_ref.at[at, pl.ds(me * pack, pack)],
            send_sem=send_sem.at[at],
            recv_sem=recv_sem.at[at],
            device_id=where,
            device_id_type=MESH,
        ).start()

    def send_all(at):
        groups = devices // GROUP

        @pl.loop(0, groups - 1)
        def _(group):
            for item in range(GROUP):
                make_out(at, group * GROUP + item)
            for item in range(GROUP):
                send(at, group * GROUP + item)

        for index in range(devices - GROUP, devices - 1):
            make_out(at, index)
        for index in range(devices - GROUP, devices - 1):
            send(at, index)
        make(at, me, arrived_ref, me * pack)

    def gather_in(at, names, first, count):
        ids = lax.broadcasted_iota(jnp.int32, (count * slots, devices), 0) + (first * slots + 1)
        hits = [
            (ids == names[at * CAP + copy_at : at * CAP + copy_at + 1, :])
            .astype(jnp.float32)
            .astype(jnp.bfloat16)
            for copy_at in range(CAP)
        ]
        placer = jnp.concatenate(hits + hits, axis=1)
        for r in range(rhs):
            rows = [
                arrived_ref[at, pl.ds(copy_at * rhs + r, devices, stride=pack), :]
                for copy_at in range(CAP)
            ]
            high = [row.astype(jnp.bfloat16) for row in rows]
            low = [
                (row - top.astype(jnp.float32)).astype(jnp.bfloat16)
                for row, top in zip(rows, high)
            ]
            total = jnp.dot(
                placer,
                jnp.concatenate(high + low, axis=0),
                preferred_element_type=jnp.float32,
            )
            where = pl.ds(first * level_rows + r, count * slots, stride=rhs)
            work_ref[where, :] = work_ref[where, :] - total

    right_load.wait()
    solve(0)
    record_copy.wait()
    off_loads[0].wait()
    pl.semaphore_wait(barrier, devices - 1)

    @pl.loop(0, devices - 1)
    def _(index):
        other, where = partner(index)
        pltpu.make_async_remote_copy(
            src_ref=names_out_ref.at[pl.ds(other, 1)],
            dst_ref=names_ref.at[pl.ds(me, 1)],
            send_sem=name_send_sem,
            recv_sem=name_recv_sem,
            device_id=where,
            device_id_type=MESH,
        ).start()

    send_all(0)
    name_part = names_ref.at[pl.ds(0, devices - 1)]
    pltpu.make_async_copy(name_part, name_part, name_recv_sem).wait()
    wanted = -(-(levels - 1) * CAP // 8) * 8
    pick = (
        lax.broadcasted_iota(jnp.int32, (wanted, lanes), 0)
        == lax.broadcasted_iota(jnp.int32, (wanted, lanes), 1)
    ).astype(jnp.float32)
    names = lax.dot_general(
        pick,
        names_ref[...].reshape(devices, lanes),
        (((1,), (1,)), ((), ())),
        preferred_element_type=jnp.float32,
        precision=lax.Precision.HIGHEST,
    ).astype(jnp.int32)

    for at in range(1, levels):
        incoming = arrived_ref.at[at - 1, pl.ds(0, (devices - 1) * pack)]
        pltpu.make_async_copy(incoming, incoming, recv_sem.at[at - 1]).wait()
        gather_in(at - 1, names, at, 1)
        solve(at)
        if at < levels - 1:
            off_loads[at].wait()
            send_all(at)
            gather_in(at - 1, names, at + 1, levels - 1 - at)

    for at in range(levels):
        pltpu.make_async_copy(solved_ref.at[at], out_hbm.at[at], out_sem.at[at]).wait()
    name_part = names_out_ref.at[pl.ds(0, devices - 1)]
    pltpu.make_async_copy(name_part, name_part, name_send_sem).wait()
    for at in range(levels - 1):
        part = outgoing_ref.at[at, pl.ds(0, (devices - 1) * pack)]
        pltpu.make_async_copy(part, part, send_sem.at[at]).wait()


def shards(
    sizes,
    right_side,
    diag_inverse,
    off_blocks,
    live_counts,
    source_slot,
    target_owner,
    target_block,
):
    levels, slots, rhs, width = right_side.shape
    records = off_blocks.shape[1]
    devices = sizes[0] * sizes[1] * sizes[2]
    arrivals = devices * CAP
    lanes = 128
    smem = pl.BlockSpec(memory_space=pltpu.SMEM)
    vmem = pl.BlockSpec(memory_space=pltpu.VMEM)
    anywhere = pl.BlockSpec(memory_space=pl.ANY)
    return pl.pallas_call(
        functools.partial(kernel, sizes),
        out_shape=jax.ShapeDtypeStruct((levels, slots, rhs, width), jnp.float32),
        in_specs=[smem, smem, vmem, vmem, anywhere, anywhere, anywhere],
        out_specs=anywhere,
        scratch_shapes=[
            pltpu.VMEM((levels * slots * rhs, width), jnp.float32),
            pltpu.VMEM(diag_inverse.shape, diag_inverse.dtype),
            tuple(
                pltpu.VMEM(off_blocks.shape[1:], off_blocks.dtype) for _ in range(levels - 1)
            ),
            pltpu.VMEM((levels, slots, rhs, width), jnp.float32),
            pltpu.VMEM((levels - 1, arrivals * rhs, width), jnp.float32),
            pltpu.VMEM((levels - 1, arrivals * rhs, width), jnp.float32),
            pltpu.VMEM((devices, 1, lanes), jnp.float32),
            pltpu.VMEM((devices, 1, lanes), jnp.float32),
            pltpu.VMEM((devices, lanes), jnp.int32),
            pltpu.SMEM((devices, lanes), jnp.int32),
            pltpu.SemaphoreType.DMA((2 * levels,)),
            pltpu.SemaphoreType.DMA((levels,)),
            pltpu.SemaphoreType.DMA,
            pltpu.SemaphoreType.DMA((levels - 1,)),
            pltpu.SemaphoreType.DMA((levels - 1,)),
            pltpu.SemaphoreType.DMA,
            pltpu.SemaphoreType.DMA,
        ],
        compiler_params=pltpu.CompilerParams(
            collective_id=0, has_side_effects=True, vmem_limit_bytes=60 * 1024 * 1024
        ),
    )(
        live_counts.reshape(1, levels),
        source_slot,
        target_owner,
        target_block,
        right_side.reshape(levels * slots * rhs, width),
        diag_inverse,
        off_blocks,
    )


def solution(mesh):
    sizes = tuple(mesh.shape[axis] for axis in AXES)
    in_specs = (
        P(None, AXES, None, None),
        P(None, AXES, None, None),
        P(None, AXES, None, None),
        P(None, AXES),
        P(None, AXES),
        P(None, AXES),
        P(None, AXES),
    )
    return jax.shard_map(
        functools.partial(shards, sizes),
        mesh=mesh,
        in_specs=in_specs,
        out_specs=P(None, AXES, None, None),
        check_vma=False,
    )
```

profile of v0, /device:TPU:0, one launch (start us, length us, event | category | flops | bytes accessed | tf_op | source)
XLA Modules:
  0.0 43.5 jit_solution(12261662498209413027)
XLA Ops:
  0.0 41.7 %shard_map.73 = f32[5,16,8,128]{3,2,1,0:T(8,128)} custom-call(s32[1,5]{1,0:T(1,128)} %bitcast.3, s32[4,32]{1,0:T(4,128)} %source_ref.1, s32[4,32]{1,0:T(4,128)} %owner_ref.1, s32[4,32]{1,0:T(4,128)} %block_ref.1, f32[640,128]{1,0:T(8,128)} %bitcast.2, bf16[5,16,128,128]{3,2,1,0:T(8,128)(2,1)} %diag_hbm.1, bf16[4,32,128,128]{3,2,1,0:T(8,128)(2,1)} %off_hbm.1), custom_call_target="tpu_custom_call" | custom-call | tf_op jit(solution)/shard_map/pallas_call | solution.py:256
  41.8 1.7 %copy.9 = f32[5,16,8,128]{3,2,1,0:T(8,128)} copy(f32[5,16,8,128]{3,2,1,0:T(8,128)} %shard_map.73) | data formatting | bytes 655360
where the time goes:
time: 43.6 us; the launch traced here: 43.5 us
  Pallas kernels  41.7 us (96%)
  local copies, waits for them, and re-layouts  1.72 us (4%)
    pallas_call x1, Pallas kernels, shards(): pl.pallas_call(functools.partial(kernel, sizes), out_shape=jax.ShapeDtype...  41.7 us
    unnamed x1, local copies, waits for them, and re-layouts  1.72 us

commit v1 on v0

v1 whole, which is shorter than its diff:
```python
import functools

import jax
import jax.numpy as jnp
from jax import lax
from jax.experimental import pallas as pl
from jax.experimental.pallas import tpu as pltpu
from jax.sharding import PartitionSpec as P

CAP = 2
GROUPS = 4
CHUNK = 32
TILE = 8
AXES = ("gx", "gy", "gz")
MESH = pl.DeviceIdType.MESH


def kernel(
    sizes,
    live_hbm,
    source_hbm,
    owner_hbm,
    block_hbm,
    right_hbm,
    diag_hbm,
    off_hbm,
    out_ref,
    live_ref,
    source_ref,
    owner_ref,
    block_ref,
    right_ref,
    work_ref,
    diag_ref,
    off_refs,
    solved_ref,
    made_ref,
    outgoing_ref,
    arrived_ref,
    placer_ref,
    names_out_ref,
    names_ref,
    record_vmem,
    record_ref,
    small_sem,
    load_sem,
    record_sem,
    send_sem,
    recv_sem,
    name_send_sem,
    name_recv_sem,
):
    nx, ny, nz = sizes
    devices = nx * ny * nz
    plane = nx * nz
    levels, slots = diag_ref.shape[:2]
    records = off_refs[0].shape[0]
    lanes = names_ref.shape[-1]
    groups = work_ref.shape[1]
    rows = TILE // groups
    pack = CAP * rows
    mx, my, mz = (lax.axis_index(axis) for axis in AXES)
    me = (mx * ny + my) * nz + mz

    def partner(index):
        at = index // plane
        down = ny - 1 - at
        down = down - jnp.where(down > my, 0, 1)
        up = at + jnp.where(at < my, 0, 1)
        oy = jnp.where(at == ny - 1, my, jnp.where(2 * my < ny, down, up))
        rest = index % plane + 1
        ox = lax.rem(mx + rest // nz, nx)
        oz = lax.rem(mz + rest % nz, nz)
        return (ox * ny + oy) * nz + oz, (ox, oy, oz)

    def over(count, body):
        whole = count // CHUNK if count > CHUNK else 0

        if whole:

            @pl.loop(0, whole)
            def _(chunk):
                for item in range(CHUNK):
                    body(chunk * CHUNK + item)

        for index in range(whole * CHUNK, count):
            body(index)

    def over_partners(body):
        over(devices - 1, body)

    smalls = [
        pltpu.make_async_copy(live_hbm, live_ref, small_sem.at[0]),
        pltpu.make_async_copy(source_hbm, source_ref, small_sem.at[1]),
        pltpu.make_async_copy(owner_hbm, owner_ref, small_sem.at[2]),
        pltpu.make_async_copy(block_hbm, block_ref, small_sem.at[3]),
    ]
    right_load = pltpu.make_async_copy(right_hbm, right_ref, load_sem.at[0])
    diag_loads = [
        pltpu.make_async_copy(diag_hbm.at[at], diag_ref.at[at], load_sem.at[1 + at])
        for at in range(levels)
    ]
    off_loads = [
        pltpu.make_async_copy(off_hbm.at[at], off_refs[at], load_sem.at[1 + levels + at])
        for at in range(levels - 1)
    ]
    barrier = pltpu.get_barrier_semaphore()

    for copy in reversed(smalls):
        copy.start()
    right_load.start()
    diag_loads[0].start()
    off_loads[0].start()

    def greet(index):
        pl.semaphore_signal(barrier, inc=1, device_id=partner(index)[1], device_id_type=MESH)

    over_partners(greet)
    for at in range(1, levels):
        diag_loads[at].start()
        if at < levels - 1:
            off_loads[at].start()

    tile_rows = lax.broadcasted_iota(jnp.int32, (TILE, lanes), 0)

    def spread(at):
        for group in range(groups):
            for slot in range(slots):
                base = (at * slots + slot) * TILE + group * rows
                value = None
                for r in reversed(range(rows)):
                    row = jnp.broadcast_to(right_ref[base + r : base + r + 1, :], (TILE, lanes))
                    value = row if value is None else jnp.where(tile_rows % rows == r, row, value)
                work_ref[at, group, slot * TILE : (slot + 1) * TILE, :] = value

    def solve(at, group, total):
        count = live_ref[0, at]
        for slot in range(slots):
            part = slice(slot * TILE, (slot + 1) * TILE)
            work = work_ref[at, group, part, :]
            if total is not None:
                work = work - total[part]
            solved = jnp.dot(
                work.astype(jnp.bfloat16), diag_ref[at, slot], preferred_element_type=jnp.float32
            )
            solved = jnp.where(slot < count, solved, jnp.float32(0.0))
            solved_ref[slot] = solved
            out_ref[at, slot] = jnp.where(tile_rows // rows == group, solved, out_ref[at, slot])

    def make(at, group):
        for record in range(records):
            picked = solved_ref[source_ref[at, record]].astype(jnp.bfloat16)
            made_ref[record] = jnp.dot(
                picked, off_refs[at][record], preferred_element_type=jnp.float32
            )

        def message(other):
            first, last = (made_ref[record_ref[other, at * CAP + c]] for c in range(CAP))
            return jnp.where(tile_rows % pack < rows, first, last)

        def place(tile):
            value = None
            for item in range(TILE // pack):
                part = message(partner(tile * (TILE // pack) + item)[0])
                value = part if item == 0 else jnp.where(tile_rows // pack < item, value, part)
            outgoing_ref[at, group, pl.ds(tile * TILE, TILE), :] = value

        over(devices * pack // TILE, place)
        arrived_ref[at, group, pl.ds(me * pack, pack), :] = message(me)[:pack]

    def send(at, group):
        def one(index):
            _, where = partner(index)
            pltpu.make_async_remote_copy(
                src_ref=outgoing_ref.at[at, group, pl.ds(index * pack, pack)],
                dst_ref=arrived_ref.at[at, group, pl.ds(me * pack, pack)],
                send_sem=send_sem.at[at, group],
                recv_sem=recv_sem.at[at, group],
                device_id=where,
                device_id_type=MESH,
            ).start()

        over_partners(one)

    def incoming(at, group):
        value = arrived_ref[at, group]
        high = value.astype(jnp.bfloat16)
        low = (value - high.astype(jnp.float32)).astype(jnp.bfloat16)
        return jnp.concatenate([high, low], axis=0)

    def pair_at(source, target):
        return sum(levels - 1 - at for at in range(source)) + target - source - 1

    def gather(source, target, values):
        placer = placer_ref[pair_at(source, target)]
        return jnp.dot(
            jnp.concatenate([placer, placer], axis=1), values, preferred_element_type=jnp.float32
        )

    smalls[2].wait()
    smalls[3].wait()
    owner_ids = lax.broadcasted_iota(jnp.int32, (devices, records), 0)
    record_ids = lax.broadcasted_iota(jnp.int32, (devices, records), 1)
    lane_ids = lax.broadcasted_iota(jnp.int32, (devices, lanes), 1)
    told = jnp.zeros((devices, lanes), jnp.float32)
    index = jnp.zeros((devices, lanes), jnp.int32)
    for at in range(levels - 1):
        hits = owner_ids == owner_ref[at : at + 1, :]
        block_row = (block_ref[at : at + 1, :] + 1).astype(jnp.float32)
        first = jnp.min(jnp.where(hits, record_ids, records - 1), axis=1, keepdims=True)
        last = jnp.max(jnp.where(hits, record_ids, 0), axis=1, keepdims=True)
        for copy_at, record in enumerate((first, last)):
            chosen = jnp.where(hits & (record_ids == record), block_row, 0.0)
            label = jnp.sum(chosen, axis=1, keepdims=True)
            told = jnp.where(lane_ids == at * CAP + copy_at, label, told)
            index = jnp.where(lane_ids == at * CAP + copy_at, record, index)
    record_vmem[...] = index
    record_copy = pltpu.make_async_copy(record_vmem, record_ref, record_sem)
    record_copy.start()
    names_out_ref[...] = told.reshape(devices, 1, lanes)
    names_ref[pl.ds(me, 1)] = names_out_ref[pl.ds(me, 1)]

    right_load.wait()
    spread(0)
    smalls[0].wait()
    smalls[1].wait()
    diag_loads[0].wait()
    off_loads[0].wait()
    record_copy.wait()

    solve(0, 0, None)
    make(0, 0)
    pl.semaphore_wait(barrier, devices - 1)

    def tell(index):
        other, where = partner(index)
        pltpu.make_async_remote_copy(
            src_ref=names_out_ref.at[pl.ds(other, 1)],
            dst_ref=names_ref.at[pl.ds(me, 1)],
            send_sem=name_send_sem,
            recv_sem=name_recv_sem,
            device_id=where,
            device_id_type=MESH,
        ).start()

    over_partners(tell)

    send(0, 0)

    @pl.loop(1, groups)
    def _(group):
        solve(0, group, None)
        make(0, group)
        send(0, group)

    for at in range(1, levels):
        spread(at)

    name_part = names_ref.at[pl.ds(0, devices - 1)]
    pltpu.make_async_copy(name_part, name_part, name_recv_sem).wait()
    width = devices * pack
    wanted = -(-(levels - 1) * CAP // 8) * 8
    pick = (
        lax.broadcasted_iota(jnp.int32, (wanted, lanes), 0)
        == lax.broadcasted_iota(jnp.int32, (wanted, lanes), 1)
    ).astype(jnp.float32)
    names = lax.dot_general(
        pick,
        names_ref[...].reshape(devices, lanes),
        (((1,), (1,)), ((), ())),
        preferred_element_type=jnp.float32,
        precision=lax.Precision.HIGHEST,
    )
    widen = (
        lax.broadcasted_iota(jnp.int32, (devices, width), 0)
        == lax.broadcasted_iota(jnp.int32, (devices, width), 1) // pack
    ).astype(jnp.float32)
    wide = jnp.dot(
        names, widen, preferred_element_type=jnp.float32, precision=lax.Precision.HIGHEST
    ).astype(jnp.int32)
    column = lax.broadcasted_iota(jnp.int32, (1, width), 1)
    height = slots * TILE
    row_ids = lax.broadcasted_iota(jnp.int32, (height, width), 0)
    same = row_ids % rows == lax.broadcasted_iota(jnp.int32, (height, width), 1) % rows
    slot_ids = row_ids // TILE
    for source in range(levels - 1):
        at = source * CAP
        label = wide[at : at + 1]
        for c in range(1, CAP):
            label = jnp.where(column % pack // rows == c, wide[at + c : at + c + 1], label)
        for target in range(source + 1, levels):
            hit = same & (slot_ids == label - (target * slots + 1))
            placer_ref[pair_at(source, target)] = hit.astype(jnp.float32).astype(jnp.bfloat16)

    for at in range(1, levels):
        diag_loads[at].wait()
        if at < levels - 1:
            off_loads[at].wait()

        @pl.loop(0, groups)
        def _(group):
            part = arrived_ref.at[at - 1, group, pl.ds(0, (devices - 1) * pack)]
            pltpu.make_async_copy(part, part, recv_sem.at[at - 1, group]).wait()
            values = incoming(at - 1, group)
            solve(at, group, gather(at - 1, at, values))
            if at < levels - 1:
                make(at, group)
                send(at, group)
                for target in range(at + 1, levels):
                    work_ref[target, group] = work_ref[target, group] - gather(
                        at - 1, target, values
                    )

    name_part = names_out_ref.at[pl.ds(0, devices - 1)]
    pltpu.make_async_copy(name_part, name_part, name_send_sem).wait()
    for at in range(levels - 1):
        for group in range(groups):
            part = outgoing_ref.at[at, group, pl.ds(0, (devices - 1) * pack)]
            pltpu.make_async_copy(part, part, send_sem.at[at, group]).wait()


def shards(
    sizes,
    right_side,
    diag_inverse,
    off_blocks,
    live_counts,
    source_slot,
    target_owner,
    target_block,
):
    levels, slots, rhs, width = right_side.shape
    records = off_blocks.shape[1]
    devices = sizes[0] * sizes[1] * sizes[2]
    lanes = 128
    pack = CAP * rhs // GROUPS
    pairs = levels * (levels - 1) // 2
    vmem = pl.BlockSpec(memory_space=pltpu.VMEM)
    anywhere = pl.BlockSpec(memory_space=pl.ANY)
    messages = (levels - 1, GROUPS, devices * pack, width)
    return pl.pallas_call(
        functools.partial(kernel, sizes),
        out_shape=pltpu.VMEM((levels, slots, rhs, width), jnp.float32),
        in_specs=[anywhere] * 7,
        out_specs=vmem,
        scratch_shapes=[
            pltpu.SMEM((1, levels), jnp.int32),
            pltpu.SMEM(source_slot.shape, jnp.int32),
            pltpu.VMEM(target_owner.shape, jnp.int32),
            pltpu.VMEM(target_block.shape, jnp.int32),
            pltpu.VMEM((levels * slots * rhs, width), jnp.float32),
            pltpu.VMEM((levels, GROUPS, slots * rhs, width), jnp.float32),
            pltpu.VMEM(diag_inverse.shape, diag_inverse.dtype),
            tuple(
                pltpu.VMEM(off_blocks.shape[1:], off_blocks.dtype) for _ in range(levels - 1)
            ),
            pltpu.VMEM((slots, rhs, width), jnp.float32),
            pltpu.VMEM((records, rhs, width), jnp.float32),
            pltpu.VMEM(messages, jnp.float32),
            pltpu.VMEM(messages, jnp.float32),
            pltpu.VMEM((pairs, slots * rhs, devices * pack), jnp.bfloat16),
            pltpu.VMEM((devices, 1, lanes), jnp.float32),
            pltpu.VMEM((devices, 1, lanes), jnp.float32),
            pltpu.VMEM((devices, lanes), jnp.int32),
            pltpu.SMEM((devices, lanes), jnp.int32),
            pltpu.SemaphoreType.DMA((4,)),
            pltpu.SemaphoreType.DMA((2 * levels,)),
            pltpu.SemaphoreType.DMA,
            pltpu.SemaphoreType.DMA((levels - 1, GROUPS)),
            pltpu.SemaphoreType.DMA((levels - 1, GROUPS)),
            pltpu.SemaphoreType.DMA,
            pltpu.SemaphoreType.DMA,
        ],
        compiler_params=pltpu.CompilerParams(
            collective_id=0, has_side_effects=True, vmem_limit_bytes=60 * 1024 * 1024
        ),
    )(
        live_counts.reshape(1, levels),
        source_slot,
        target_owner,
        target_block,
        right_side.reshape(levels * slots * rhs, width),
        diag_inverse,
        off_blocks,
    )


def solution(mesh):
    sizes = tuple(mesh.shape[axis] for axis in AXES)
    in_specs = (
        P(None, AXES, None, None),
        P(None, AXES, None, None),
        P(None, AXES, None, None),
        P(None, AXES),
        P(None, AXES),
        P(None, AXES),
        P(None, AXES),
    )
    return jax.shard_map(
        functools.partial(shards, sizes),
        mesh=mesh,
        in_specs=in_specs,
        out_specs=P(None, AXES, None, None),
        check_vma=False,
    )
```

time: 43.6 us -> 34.6 us (0.79)
  Pallas kernels: 41.7 us -> 33.7 us
  local copies, waits for them, and re-layouts: 1.72 us -> 0.73 us
    pallas_call x1, Pallas kernels: 41.7 us -> 33.7 us  [shards(): pl.pallas_call(functools.partial(kernel, sizes), out_shape=pltpu.VMEM((le...]
    unnamed x1, local copies, waits for them, and re-layouts: 1.72 us -> 0.73 us
where the time goes in v1:
time: 34.6 us; the launch traced here: 34.4 us
  Pallas kernels  33.7 us (97%)
  local copies, waits for them, and re-layouts  0.73 us (2%)
    pallas_call x1, Pallas kernels, shards(): pl.pallas_call(functools.partial(kernel, sizes), out_shape=pltpu.VMEM((le...  33.7 us
    unnamed x1, local copies, waits for them, and re-layouts  0.73 us

profile of v1, /device:TPU:0, one launch (start us, length us, event | category | flops | bytes accessed | tf_op | source)
XLA Modules:
  0.0 34.4 jit_solution(10322687554124205311)
XLA Ops:
  0.0 33.7 %shard_map.73 = f32[5,16,8,128]{3,2,1,0:T(8,128)S(1)} custom-call(s32[1,5]{1,0:T(1,128)} %bitcast.3, s32[4,32]{1,0:T(4,128)} %source_hbm.1, s32[4,32]{1,0:T(4,128)} %owner_hbm.1, s32[4,32]{1,0:T(4,128)} %block_hbm.1, f32[640,128]{1,0:T(8,128)} %bitcast.2, bf16[5,16,128,128]{3,2,1,0:T(8,128)(2,1)} %diag_hbm.1, bf16[4,32,128,128]{3,2,1,0:T(8,128)(2,1)} %off_hbm.1), custom_call_target="tpu_custom_call" | custom-call | tf_op jit(solution)/shard_map/pallas_call | solution.py:341
  33.7 0.7 %copy.9 = f32[5,16,8,128]{3,2,1,0:T(8,128)} copy(f32[5,16,8,128]{3,2,1,0:T(8,128)S(1)} %shard_map.73) | data formatting | bytes 655360

commit v2 on v1

--- a/solution.py
+++ b/solution.py
@@ -9,10 +9,18 @@
 
 CAP = 2
 GROUPS = 4
-CHUNK = 32
 TILE = 8
 AXES = ("gx", "gy", "gz")
 MESH = pl.DeviceIdType.MESH
+
+
+def shifted(coord, offset, size):
+    if size & (size - 1):
+        return (coord + offset) % size
+    for bit in range(size.bit_length() - 1):
+        if offset >> bit & 1:
+            coord = coord + (1 << bit) * (1 - 2 * (coord // (1 << bit) % 2))
+    return coord
 
 
 def kernel(
@@ -32,7 +40,7 @@
     right_ref,
     work_ref,
     diag_ref,
-    off_refs,
+    off_ref,
     solved_ref,
     made_ref,
     outgoing_ref,
@@ -44,7 +52,6 @@
     record_ref,
     small_sem,
     load_sem,
-    record_sem,
     send_sem,
     recv_sem,
     name_send_sem,
@@ -52,9 +59,8 @@
 ):
     nx, ny, nz = sizes
     devices = nx * ny * nz
-    plane = nx * nz
     levels, slots = diag_ref.shape[:2]
-    records = off_refs[0].shape[0]
+    records = off_ref.shape[1]
     lanes = names_ref.shape[-1]
     groups = work_ref.shape[1]
     rows = TILE // groups
@@ -62,28 +68,18 @@
     mx, my, mz = (lax.axis_index(axis) for axis in AXES)
     me = (mx * ny + my) * nz + mz
 
+    coords = [[shifted(m, d, n) for d in range(n)] for m, n in zip((mx, my, mz), sizes)]
+    offsets = sorted(
+        [(dx, dy, dz) for dx in range(nx) for dy in range(ny) for dz in range(nz)],
+        key=lambda o: (-o[1].bit_count() - (o[1] > 2) - o[0].bit_count(), -o[1], -o[0], -o[2]),
+    )
+
     def partner(index):
-        at = index // plane
-        down = ny - 1 - at
-        down = down - jnp.where(down > my, 0, 1)
-        up = at + jnp.where(at < my, 0, 1)
-        oy = jnp.where(at == ny - 1, my, jnp.where(2 * my < ny, down, up))
-        rest = index % plane + 1
-        ox = lax.rem(mx + rest // nz, nx)
-        oz = lax.rem(mz + rest % nz, nz)
-        return (ox * ny + oy) * nz + oz, (ox, oy, oz)
+        where = tuple(coord[d] for coord, d in zip(coords, offsets[index]))
+        return (where[0] * ny + where[1]) * nz + where[2], where
 
     def over(count, body):
-        whole = count // CHUNK if count > CHUNK else 0
-
-        if whole:
-
-            @pl.loop(0, whole)
-            def _(chunk):
-                for item in range(CHUNK):
-                    body(chunk * CHUNK + item)
-
-        for index in range(whole * CHUNK, count):
+        for index in range(count):
             body(index)
 
     def over_partners(body):
@@ -96,31 +92,27 @@
         pltpu.make_async_copy(block_hbm, block_ref, small_sem.at[3]),
     ]
     right_load = pltpu.make_async_copy(right_hbm, right_ref, load_sem.at[0])
-    diag_loads = [
-        pltpu.make_async_copy(diag_hbm.at[at], diag_ref.at[at], load_sem.at[1 + at])
-        for at in range(levels)
-    ]
-    off_loads = [
-        pltpu.make_async_copy(off_hbm.at[at], off_refs[at], load_sem.at[1 + levels + at])
-        for at in range(levels - 1)
-    ]
+    first_loads, rest_loads = (
+        [
+            pltpu.make_async_copy(hbm.at[part], ref.at[part], load_sem.at[1 + i])
+            for i, (hbm, ref, count) in enumerate(
+                ((diag_hbm, diag_ref, levels), (off_hbm, off_ref, levels - 1))
+            )
+            for part in (pl.ds(begin, 1 if begin == 0 else count - 1),)
+        ]
+        for begin in (0, 1)
+    )
     barrier = pltpu.get_barrier_semaphore()
+
+    def greet(index):
+        pl.semaphore_signal(barrier, inc=1, device_id=partner(index)[1], device_id_type=MESH)
 
     for copy in reversed(smalls):
         copy.start()
     right_load.start()
-    diag_loads[0].start()
-    off_loads[0].start()
-
-    def greet(index):
-        pl.semaphore_signal(barrier, inc=1, device_id=partner(index)[1], device_id_type=MESH)
-
+    for copy in first_loads:
+        copy.start()
     over_partners(greet)
-    for at in range(1, levels):
-        diag_loads[at].start()
-        if at < levels - 1:
-            off_loads[at].start()
-
     tile_rows = lax.broadcasted_iota(jnp.int32, (TILE, lanes), 0)
 
     def spread(at):
@@ -147,12 +139,15 @@
             solved_ref[slot] = solved
             out_ref[at, slot] = jnp.where(tile_rows // rows == group, solved, out_ref[at, slot])
 
-    def make(at, group):
+    def make(at, group, awaited=None):
         for record in range(records):
             picked = solved_ref[source_ref[at, record]].astype(jnp.bfloat16)
             made_ref[record] = jnp.dot(
-                picked, off_refs[at][record], preferred_element_type=jnp.float32
+                picked, off_ref[at, record], preferred_element_type=jnp.float32
             )
+
+        if awaited is not None:
+            awaited.wait()
 
         def message(other):
             first, last = (made_ref[record_ref[other, at * CAP + c]] for c in range(CAP))
@@ -174,8 +169,8 @@
             pltpu.make_async_remote_copy(
                 src_ref=outgoing_ref.at[at, group, pl.ds(index * pack, pack)],
                 dst_ref=arrived_ref.at[at, group, pl.ds(me * pack, pack)],
-                send_sem=send_sem.at[at, group],
-                recv_sem=recv_sem.at[at, group],
+                send_sem=send_sem.at[group],
+                recv_sem=recv_sem.at[at % 2, group],
                 device_id=where,
                 device_id_type=MESH,
             ).start()
@@ -215,7 +210,7 @@
             told = jnp.where(lane_ids == at * CAP + copy_at, label, told)
             index = jnp.where(lane_ids == at * CAP + copy_at, record, index)
     record_vmem[...] = index
-    record_copy = pltpu.make_async_copy(record_vmem, record_ref, record_sem)
+    record_copy = pltpu.make_async_copy(record_vmem, record_ref, small_sem.at[2])
     record_copy.start()
     names_out_ref[...] = told.reshape(devices, 1, lanes)
     names_ref[pl.ds(me, 1)] = names_out_ref[pl.ds(me, 1)]
@@ -224,12 +219,13 @@
     spread(0)
     smalls[0].wait()
     smalls[1].wait()
-    diag_loads[0].wait()
-    off_loads[0].wait()
-    record_copy.wait()
+    for copy in first_loads:
+        copy.wait()
+    for copy in rest_loads:
+        copy.start()
 
     solve(0, 0, None)
-    make(0, 0)
+    make(0, 0, record_copy)
     pl.semaphore_wait(barrier, devices - 1)
 
     def tell(index):
@@ -269,21 +265,19 @@
         names_ref[...].reshape(devices, lanes),
         (((1,), (1,)), ((), ())),
         preferred_element_type=jnp.float32,
-        precision=lax.Precision.HIGHEST,
     )
     widen = (
         lax.broadcasted_iota(jnp.int32, (devices, width), 0)
         == lax.broadcasted_iota(jnp.int32, (devices, width), 1) // pack
     ).astype(jnp.float32)
-    wide = jnp.dot(
-        names, widen, preferred_element_type=jnp.float32, precision=lax.Precision.HIGHEST
-    ).astype(jnp.int32)
+    wide = jnp.dot(names, widen, preferred_element_type=jnp.float32).astype(jnp.int32)
     column = lax.broadcasted_iota(jnp.int32, (1, width), 1)
     height = slots * TILE
     row_ids = lax.broadcasted_iota(jnp.int32, (height, width), 0)
     same = row_ids % rows == lax.broadcasted_iota(jnp.int32, (height, width), 1) % rows
     slot_ids = row_ids // TILE
-    for source in range(levels - 1):
+
+    def build(source):
         at = source * CAP
         label = wide[at : at + 1]
         for c in range(1, CAP):
@@ -292,31 +286,30 @@
             hit = same & (slot_ids == label - (target * slots + 1))
             placer_ref[pair_at(source, target)] = hit.astype(jnp.float32).astype(jnp.bfloat16)
 
+    build(0)
+    for copy in rest_loads:
+        copy.wait()
+    name_part = names_out_ref.at[pl.ds(0, devices - 1)]
+    pltpu.make_async_copy(name_part, name_part, name_send_sem).wait()
     for at in range(1, levels):
-        diag_loads[at].wait()
         if at < levels - 1:
-            off_loads[at].wait()
-
+            build(at)
         @pl.loop(0, groups)
         def _(group):
             part = arrived_ref.at[at - 1, group, pl.ds(0, (devices - 1) * pack)]
-            pltpu.make_async_copy(part, part, recv_sem.at[at - 1, group]).wait()
+            pltpu.make_async_copy(part, part, recv_sem.at[(at - 1) % 2, group]).wait()
             values = incoming(at - 1, group)
-            solve(at, group, gather(at - 1, at, values))
+            total = gather(at - 1, at, values)
+            for target in range(at + 1, levels):
+                work_ref[target, group] = work_ref[target, group] - gather(
+                    at - 1, target, values
+                )
+            solve(at, group, total)
+            part = outgoing_ref.at[at - 1, group, pl.ds(0, (devices - 1) * pack)]
+            pltpu.make_async_copy(part, part, send_sem.at[group]).wait()
             if at < levels - 1:
                 make(at, group)
                 send(at, group)
-                for target in range(at + 1, levels):
-                    work_ref[target, group] = work_ref[target, group] - gather(
-                        at - 1, target, values
-                    )
-
-    name_part = names_out_ref.at[pl.ds(0, devices - 1)]
-    pltpu.make_async_copy(name_part, name_part, name_send_sem).wait()
-    for at in range(levels - 1):
-        for group in range(groups):
-            part = outgoing_ref.at[at, group, pl.ds(0, (devices - 1) * pack)]
-            pltpu.make_async_copy(part, part, send_sem.at[at, group]).wait()
 
 
 def shards(
@@ -351,9 +344,7 @@
             pltpu.VMEM((levels * slots * rhs, width), jnp.float32),
             pltpu.VMEM((levels, GROUPS, slots * rhs, width), jnp.float32),
             pltpu.VMEM(diag_inverse.shape, diag_inverse.dtype),
-            tuple(
-                pltpu.VMEM(off_blocks.shape[1:], off_blocks.dtype) for _ in range(levels - 1)
-            ),
+            pltpu.VMEM(off_blocks.shape, off_blocks.dtype),
             pltpu.VMEM((slots, rhs, width), jnp.float32),
             pltpu.VMEM((records, rhs, width), jnp.float32),
             pltpu.VMEM(messages, jnp.float32),
@@ -364,10 +355,9 @@
             pltpu.VMEM((devices, lanes), jnp.int32),
             pltpu.SMEM((devices, lanes), jnp.int32),
             pltpu.SemaphoreType.DMA((4,)),
-            pltpu.SemaphoreType.DMA((2 * levels,)),
-            pltpu.SemaphoreType.DMA,
-            pltpu.SemaphoreType.DMA((levels - 1, GROUPS)),
-            pltpu.SemaphoreType.DMA((levels - 1, GROUPS)),
+            pltpu.SemaphoreType.DMA((3,)),
+            pltpu.SemaphoreType.DMA((GROUPS,)),
+            pltpu.SemaphoreType.DMA((2, GROUPS)),
             pltpu.SemaphoreType.DMA,
             pltpu.SemaphoreType.DMA,
         ],

time: 34.6 us -> 34.3 us (level)
  no operation moved by 1% of the time
where the time goes in v2:
time: 34.3 us; the launch traced here: 34.1 us
  Pallas kernels  33.4 us (97%)
  local copies, waits for them, and re-layouts  0.73 us (2%)
    pallas_call x1, Pallas kernels, shards(): pl.pallas_call(functools.partial(kernel, sizes), out_shape=pltpu.VMEM((le...  33.4 us
    unnamed x1, local copies, waits for them, and re-layouts  0.73 us

profile of v2, /device:TPU:0, one launch (start us, length us, event | category | flops | bytes accessed | tf_op | source)
XLA Modules:
  0.0 34.1 jit_solution(6160789631588496610)
XLA Ops:
  0.0 33.4 %shard_map.73 = f32[5,16,8,128]{3,2,1,0:T(8,128)S(1)} custom-call(s32[1,5]{1,0:T(1,128)} %bitcast.3, s32[4,32]{1,0:T(4,128)} %source_hbm.1, s32[4,32]{1,0:T(4,128)} %owner_hbm.1, s32[4,32]{1,0:T(4,128)} %block_hbm.1, f32[640,128]{1,0:T(8,128)} %bitcast.2, bf16[5,16,128,128]{3,2,1,0:T(8,128)(2,1)} %diag_hbm.1, bf16[4,32,128,128]{3,2,1,0:T(8,128)(2,1)} %off_hbm.1), custom_call_target="tpu_custom_call" | custom-call | tf_op jit(solution)/shard_map/pallas_call | solution.py:334
  33.4 0.7 %copy.9 = f32[5,16,8,128]{3,2,1,0:T(8,128)} copy(f32[5,16,8,128]{3,2,1,0:T(8,128)S(1)} %shard_map.73) | data formatting | bytes 655360

commit v3 on v2

--- a/solution.py
+++ b/solution.py
@@ -71,7 +71,7 @@
     coords = [[shifted(m, d, n) for d in range(n)] for m, n in zip((mx, my, mz), sizes)]
     offsets = sorted(
         [(dx, dy, dz) for dx in range(nx) for dy in range(ny) for dz in range(nz)],
-        key=lambda o: (-o[1].bit_count() - (o[1] > 2) - o[0].bit_count(), -o[1], -o[0], -o[2]),
+        key=lambda o: (-min(o[1], 2) - o[0].bit_count(), -o[1], -o[0], -o[2]),
     )
 
     def partner(index):

time: 34.3 us -> 33.9 us (0.988)
  Pallas kernels: 33.4 us -> 33 us
    pallas_call x1, Pallas kernels: 33.4 us -> 33 us  [shards(): pl.pallas_call(functools.partial(kernel, sizes), out_shape=pltpu.VMEM((le...]
where the time goes in v3:
time: 33.9 us; the launch traced here: 33.7 us
  Pallas kernels  33 us (97%)
  local copies, waits for them, and re-layouts  0.73 us (2%)
    pallas_call x1, Pallas kernels, shards(): pl.pallas_call(functools.partial(kernel, sizes), out_shape=pltpu.VMEM((le...  33 us
    unnamed x1, local copies, waits for them, and re-layouts  0.73 us

profile of v3, /device:TPU:0, one launch (start us, length us, event | category | flops | bytes accessed | tf_op | source)
XLA Modules:
  0.0 33.7 jit_solution(4426607171875284051)
XLA Ops:
  0.0 33.0 %shard_map.73 = f32[5,16,8,128]{3,2,1,0:T(8,128)S(1)} custom-call(s32[1,5]{1,0:T(1,128)} %bitcast.3, s32[4,32]{1,0:T(4,128)} %source_hbm.1, s32[4,32]{1,0:T(4,128)} %owner_hbm.1, s32[4,32]{1,0:T(4,128)} %block_hbm.1, f32[640,128]{1,0:T(8,128)} %bitcast.2, bf16[5,16,128,128]{3,2,1,0:T(8,128)(2,1)} %diag_hbm.1, bf16[4,32,128,128]{3,2,1,0:T(8,128)(2,1)} %off_hbm.1), custom_call_target="tpu_custom_call" | custom-call | tf_op jit(solution)/shard_map/pallas_call | solution.py:334
  33.0 0.7 %copy.9 = f32[5,16,8,128]{3,2,1,0:T(8,128)} copy(f32[5,16,8,128]{3,2,1,0:T(8,128)S(1)} %shard_map.73) | data formatting | bytes 655360

commit v4 on v3

--- a/solution.py
+++ b/solution.py
@@ -9,6 +9,7 @@
 
 CAP = 2
 GROUPS = 4
+BATCH = 8
 TILE = 8
 AXES = ("gx", "gy", "gz")
 MESH = pl.DeviceIdType.MESH
@@ -54,7 +55,6 @@
     load_sem,
     send_sem,
     recv_sem,
-    name_send_sem,
     name_recv_sem,
 ):
     nx, ny, nz = sizes
@@ -160,22 +160,35 @@
                 value = part if item == 0 else jnp.where(tile_rows // pack < item, value, part)
             outgoing_ref[at, group, pl.ds(tile * TILE, TILE), :] = value
 
-        over(devices * pack // TILE, place)
+        return place, message
+
+    def keep(at, group, message):
         arrived_ref[at, group, pl.ds(me * pack, pack), :] = message(me)[:pack]
 
+    def deliver(at, group, place, message):
+        step = BATCH
+        each = TILE // pack
+        for begin in range(0, devices, step):
+            for tile in range(begin // each, (begin + step) // each):
+                place(tile)
+            if begin + step >= devices:
+                keep(at, group, message)
+            for index in range(begin, min(begin + step, devices - 1)):
+                send_one(at, group, index)
+
     def send(at, group):
-        def one(index):
-            _, where = partner(index)
-            pltpu.make_async_remote_copy(
-                src_ref=outgoing_ref.at[at, group, pl.ds(index * pack, pack)],
-                dst_ref=arrived_ref.at[at, group, pl.ds(me * pack, pack)],
-                send_sem=send_sem.at[group],
-                recv_sem=recv_sem.at[at % 2, group],
-                device_id=where,
-                device_id_type=MESH,
-            ).start()
-
-        over_partners(one)
+        over_partners(functools.partial(send_one, at, group))
+
+    def send_one(at, group, index):
+        _, where = partner(index)
+        pltpu.make_async_remote_copy(
+            src_ref=outgoing_ref.at[at, group, pl.ds(index * pack, pack)],
+            dst_ref=arrived_ref.at[at, group, pl.ds(me * pack, pack)],
+            send_sem=send_sem.at[group],
+            recv_sem=recv_sem.at[at % 2, group],
+            device_id=where,
+            device_id_type=MESH,
+        ).start()
 
     def incoming(at, group):
         value = arrived_ref[at, group]
@@ -225,7 +238,9 @@
         copy.start()
 
     solve(0, 0, None)
-    make(0, 0, record_copy)
+    place, message = make(0, 0, record_copy)
+    over(devices * pack // TILE, place)
+    keep(0, 0, message)
     pl.semaphore_wait(barrier, devices - 1)
 
     def tell(index):
@@ -233,7 +248,7 @@
         pltpu.make_async_remote_copy(
             src_ref=names_out_ref.at[pl.ds(other, 1)],
             dst_ref=names_ref.at[pl.ds(me, 1)],
-            send_sem=name_send_sem,
+            send_sem=load_sem.at[0],
             recv_sem=name_recv_sem,
             device_id=where,
             device_id_type=MESH,
@@ -246,8 +261,7 @@
     @pl.loop(1, groups)
     def _(group):
         solve(0, group, None)
-        make(0, group)
-        send(0, group)
+        deliver(0, group, *make(0, group))
 
     for at in range(1, levels):
         spread(at)
@@ -290,7 +304,7 @@
     for copy in rest_loads:
         copy.wait()
     name_part = names_out_ref.at[pl.ds(0, devices - 1)]
-    pltpu.make_async_copy(name_part, name_part, name_send_sem).wait()
+    pltpu.make_async_copy(name_part, name_part, load_sem.at[0]).wait()
     for at in range(1, levels):
         if at < levels - 1:
             build(at)
@@ -308,8 +322,7 @@
             part = outgoing_ref.at[at - 1, group, pl.ds(0, (devices - 1) * pack)]
             pltpu.make_async_copy(part, part, send_sem.at[group]).wait()
             if at < levels - 1:
-                make(at, group)
-                send(at, group)
+                deliver(at, group, *make(at, group))
 
 
 def shards(
@@ -359,7 +372,6 @@
             pltpu.SemaphoreType.DMA((GROUPS,)),
             pltpu.SemaphoreType.DMA((2, GROUPS)),
             pltpu.SemaphoreType.DMA,
-            pltpu.SemaphoreType.DMA,
         ],
         compiler_params=pltpu.CompilerParams(
             collective_id=0, has_side_effects=True, vmem_limit_bytes=60 * 1024 * 1024

time: 33.9 us -> 33.9 us (level)
  no operation moved by 1% of the time
where the time goes in v4:
time: 33.9 us; the launch traced here: 33.8 us
  Pallas kernels  33 us (97%)
  local copies, waits for them, and re-layouts  0.73 us (2%)
    pallas_call x1, Pallas kernels, shards(): pl.pallas_call(functools.partial(kernel, sizes), out_shape=pltpu.VMEM((le...  33 us
    unnamed x1, local copies, waits for them, and re-layouts  0.73 us

profile of v4, /device:TPU:0, one launch (start us, length us, event | category | flops | bytes accessed | tf_op | source)
XLA Modules:
  0.0 33.8 jit_solution(14359025563975958475)
XLA Ops:
  0.0 33.0 %shard_map.73 = f32[5,16,8,128]{3,2,1,0:T(8,128)S(1)} custom-call(s32[1,5]{1,0:T(1,128)} %bitcast.3, s32[4,32]{1,0:T(4,128)} %source_hbm.1, s32[4,32]{1,0:T(4,128)} %owner_hbm.1, s32[4,32]{1,0:T(4,128)} %block_hbm.1, f32[640,128]{1,0:T(8,128)} %bitcast.2, bf16[5,16,128,128]{3,2,1,0:T(8,128)(2,1)} %diag_hbm.1, bf16[4,32,128,128]{3,2,1,0:T(8,128)(2,1)} %off_hbm.1), custom_call_target="tpu_custom_call" | custom-call | tf_op jit(solution)/shard_map/pallas_call | solution.py:347
  33.1 0.7 %copy.9 = f32[5,16,8,128]{3,2,1,0:T(8,128)} copy(f32[5,16,8,128]{3,2,1,0:T(8,128)S(1)} %shard_map.73) | data formatting | bytes 655360
